TPU v7x, 32 devices: a whole 2x2x4 slice. The times are simulated.
32 devices in a mesh: grp: 16 (over z, y, core), seq: 2 (over x).
Axes of the slice: x: 2, y: 2, z: 4, core: 2. Of those that a mesh axis runs over, the one named last changes fastest.
Arguments:
- queries: bfloat16 [8192, 4096], P(('grp', 'seq')), may hold values from -8 to 8
- keys: bfloat16 [8192, 4096], P(('grp', 'seq')), may hold values from -6 to 6
- values: bfloat16 [8192, 4096], P(('grp', 'seq')), may hold values from -6 to 6
- global_pos: int32 [64], P(('grp', 'seq')), may hold values from 0 to 127
- layout: int32 [64, 32], P(('grp', 'seq')), may hold values from 0 to 63, all different within a row
Outputs:
- attended: bfloat16 [8192, 4096], P(('grp', 'seq'))
Inputs may be any that keep to these rules, and one draw needn't show every extreme that they name: `layout`: each row lists 32 different block indices, and every block is listed by some row.
All inputs are finite; a program needn't handle non-finite values.
Results may differ from a plain program's by a relative error of at most 0.0042.
Values may be sent and summed in bfloat16 or wider, within the bound.
A program may use at most 128 MiB of HBM per device.

v0:
```python
import math

import jax
import jax.numpy as jnp
from jax import lax
from jax.sharding import PartitionSpec as P

HEADS = 32
HEAD_DIM = 128
BLOCK = 128


def shifted(value, axis, by):
    count = lax.axis_size(axis)
    pairs = [(i, i + by) for i in range(count) if 0 <= i + by < count]
    return lax.ppermute(value, axis, pairs)


def pooled(source, blocks_dev):
    blocks = source.astype(jnp.float32).reshape(blocks_dev, BLOCK, HEADS, HEAD_DIM).mean(axis=1)
    spread = jnp.mean(blocks * blocks, axis=-1, keepdims=True)
    return (
        (blocks / jnp.sqrt(spread + 1e-06))
        .reshape(blocks_dev, HEADS * HEAD_DIM)
        .astype(jnp.bfloat16)
    )


def shards(queries, keys, values, global_pos, layout):
    rows_dev, model_width = queries.shape
    blocks_dev = rows_dev // BLOCK
    devices = lax.axis_size(("grp", "seq"))
    position = lax.axis_index(("grp", "seq"))
    score_scale = 1.0 / math.sqrt(HEAD_DIM)
    summary_keys = pooled(keys, blocks_dev)
    summary_values = pooled(values, blocks_dev)
    edge_last = jnp.stack([keys[rows_dev - BLOCK :], values[rows_dev - BLOCK :]])
    edge_first = jnp.stack([keys[:BLOCK], values[:BLOCK]])
    from_left = shifted(edge_last, ("grp", "seq"), 1)
    from_right = shifted(edge_first, ("grp", "seq"), -1)
    wide_keys = jnp.concatenate([from_left[0], keys, from_right[0]], axis=0)
    wide_values = jnp.concatenate([from_left[1], values, from_right[1]], axis=0)
    window_keys = jnp.stack(
        [wide_keys[block_at * BLOCK : (block_at + 3) * BLOCK] for block_at in range(blocks_dev)]
    )
    window_values = jnp.stack(
        [wide_values[block_at * BLOCK : (block_at + 3) * BLOCK] for block_at in range(blocks_dev)]
    )
    window_keys = window_keys.reshape(blocks_dev, 3 * BLOCK, HEADS, HEAD_DIM)
    window_values = window_values.reshape(blocks_dev, 3 * BLOCK, HEADS, HEAD_DIM)
    query_blocks = queries.reshape(blocks_dev, BLOCK, HEADS, HEAD_DIM)
    scores = (
        jnp.einsum("bqhd,bkhd->bhqk", query_blocks, window_keys, preferred_element_type=jnp.float32)
        * score_scale
    )
    key_block = (
        position * blocks_dev
        + jnp.arange(blocks_dev, dtype=jnp.int32)[:, None]
        + jnp.arange(3 * BLOCK, dtype=jnp.int32)[None, :] // BLOCK
        - 1
    )
    inside = (key_block >= 0) & (key_block < devices * blocks_dev)
    scores = jnp.where(inside[:, None, None, :], scores, -jnp.inf)
    peak = jnp.max(scores, axis=-1)
    weights = jnp.exp(scores - peak[..., None])
    totals = jnp.sum(weights, axis=-1)
    numerator = jnp.einsum(
        "bhqk,bkhd->bhqd",
        weights.astype(jnp.bfloat16),
        window_values,
        preferred_element_type=jnp.float32,
    )
    is_global = jnp.arange(BLOCK, dtype=jnp.int32)[None, :] == global_pos[:, None]
    group_keys, group_values = (
        lax.all_gather(summary_keys, "seq", axis=0, tiled=True),
        lax.all_gather(summary_values, "seq", axis=0, tiled=True),
    )
    piece_keys = lax.all_gather(group_keys, "grp", axis=0, tiled=True)
    piece_values = lax.all_gather(group_values, "grp", axis=0, tiled=True)
    length = piece_keys.shape[0]
    block_ids = jnp.arange(length, dtype=jnp.int32)
    listed = jnp.any(layout[:, :, None] == block_ids[None, None, :], axis=1)
    visible = listed[:, None, :] | is_global[:, :, None]
    part_scores = (
        jnp.einsum(
            "bqhd,jhd->bhqj",
            query_blocks,
            piece_keys.reshape(length, HEADS, HEAD_DIM),
            preferred_element_type=jnp.float32,
        )
        * score_scale
    )
    part_scores = jnp.where(visible[:, None, :, :], part_scores, -jnp.inf)
    new_peak = jnp.maximum(peak, jnp.max(part_scores, axis=-1))
    factor = jnp.exp(peak - new_peak)
    part_weights = jnp.exp(part_scores - new_peak[..., None])
    totals_next = totals * factor + jnp.sum(part_weights, axis=-1)
    numerator_next = numerator * factor[..., None] + jnp.einsum(
        "bhqj,jhd->bhqd",
        part_weights.astype(jnp.bfloat16),
        piece_values.reshape(length, HEADS, HEAD_DIM),
        preferred_element_type=jnp.float32,
    )
    result = numerator_next / totals_next[..., None]
    return jnp.transpose(result, (0, 2, 1, 3)).reshape(rows_dev, model_width).astype(jnp.bfloat16)


def solution(mesh):
    in_specs = (
        P(("grp", "seq"), None),
        P(("grp", "seq"), None),
        P(("grp", "seq"), None),
        P(("grp", "seq")),
        P(("grp", "seq"), None),
    )
    out_specs = P(("grp", "seq"), None)
    return jax.shard_map(shards, mesh=mesh, in_specs=in_specs, out_specs=out_specs, check_vma=False)
```

profile of v0, /device:TPU:0, one launch (start us, length us, event | category | flops | bytes accessed | tf_op | source)
XLA Modules:
  0.0 201.6 jit_solution(7318982374215686735)
XLA Ops:
  0.0 3.3 %copy.84 = bf16[256,4096]{0,1:T(8,128)(2,1)S(1)} copy(bf16[256,4096]{1,0:T(8,128)(2,1)} %param.6) | data formatting | bytes 4194304 | tf_op args[1]
  3.3 4.1 %copy.85 = bf16[256,4096]{0,1:T(8,128)(2,1)} copy(bf16[256,4096]{1,0:T(8,128)(2,1)} %param.7) | data formatting | bytes 4194304 | tf_op args[2]
  7.4 2.0 slice_bitcast_fusion.2
  9.4 1.6 pad_maximum_fusion.1
  12.2 1.5 pad_maximum_fusion
  13.7 7.0 %collective-permute-start = (bf16[2,128,4096]{1,2,0:T(8,128)(2,1)}, bf16[2,128,4096]{1,2,0:T(8,128)(2,1)}, u32[]{:S(2)}, u32[]{:S(2)}) collective-permute-start(bf16[2,128,4096]{1,2,0:T(8,128)(2,1)} %pad_maximum_fusion), channel_id=1, source_target_pairs={{0,1},{1,2},{2,3},{3,4},{4,5},{5,6},{6,7},{7,8},{8,9},{9,10},{10,1... | collective-permute-start | bytes 6291464 | tf_op jit(solution)/shard_map/ppermute | solution.py:16
  21.2 2.4 %convert_bitcast_fusion = f32[32,8,32,128]{3,1,2,0:T(8,128)} fusion(bf16[256,4096]{1,0:T(8,128)(2,1)S(1)} %copy-done.1), kind=kLoop, calls=%fused_computation.32 | loop fusion | flops 1048576 | bytes 6291456
  24.9 82.1 %all-gather = bf16[2,2,4096]{2,1,0:T(2,128)(2,1)S(1)} all-gather(bf16[1,2,4096]{2,1,0:T(2,128)(2,1)S(1)} %reshape.201), channel_id=1, replica_groups=mesh['grp'=16,'seq'=2] {'seq'}, dimensions={0}, use_global_device_ids=true | all-gather | bytes 49152 | tf_op jit(solution)/shard_map/all_gather | solution.py:75
  106.9 23.4 %all-gather.1 = bf16[16,4,4096]{2,1,0:T(4,128)(2,1)S(1)} all-gather(bf16[1,4,4096]{2,1,0:T(4,128)(2,1)S(1)} %reshape.203), channel_id=1, replica_groups=mesh['grp'=16,'seq'=2] {'grp'}, dimensions={0}, use_global_device_ids=true | all-gather | bytes 557056 | tf_op jit(solution)/shard_map/all_gather | solution.py:78
  130.3 2.9 %copy.117 = f32[32,8,32,128]{3,2,1,0:T(8,128)S(1)} copy(f32[32,8,32,128]{3,1,2,0:T(8,128)} %convert_bitcast_fusion) | data formatting | bytes 8388608
  133.6 4.1 %copy.96 = bf16[1,256,32,128]{3,1,2,0:T(8,128)(2,1)} copy(bf16[1,256,32,128]{1,3,2,0:T(8,128)(2,1)} %bitcast.75) | data formatting | bytes 4194304 | tf_op jit(solution)/shard_map/concatenate | solution.py:42
  137.7 2.9 %copy.88 = bf16[1,256,32,128]{3,1,2,0:T(8,128)(2,1)} copy(bf16[1,256,32,128]{1,3,2,0:T(8,128)(2,1)S(1)} %bitcast.74) | data formatting | bytes 4194304 | tf_op jit(solution)/shard_map/concatenate | solution.py:41
  140.6 2.1 %copy.115 = bf16[32,8,32,128]{3,2,1,0:T(8,128)(2,1)S(1)} copy(bf16[32,8,32,128]{3,1,2,0:T(8,128)(2,1)} %bitcast.83) | data formatting | bytes 4194304
  142.7 1.5 reshape.193
  144.3 4.4 %all-gather.2 = bf16[2,2,4096]{2,1,0:T(2,128)(2,1)S(1)} all-gather(bf16[1,2,4096]{2,1,0:T(2,128)(2,1)S(1)} %reshape.205), channel_id=1, replica_groups=mesh['grp'=16,'seq'=2] {'seq'}, dimensions={0}, use_global_device_ids=true | all-gather | bytes 49152 | tf_op jit(solution)/shard_map/all_gather | solution.py:76
  148.8 18.9 %all-gather.3 = bf16[16,4,4096]{2,1,0:T(4,128)(2,1)S(1)} all-gather(bf16[1,4,4096]{2,1,0:T(4,128)(2,1)S(1)} %reshape.207), channel_id=1, replica_groups=mesh['grp'=16,'seq'=2] {'grp'}, dimensions={0}, use_global_device_ids=true | all-gather | bytes 557056 | tf_op jit(solution)/shard_map/all_gather | solution.py:79
  168.6 3.8 %fusion.54 = (f32[2,32,128]{2,0,1:T(2,128)S(1)}, f32[2,32,128,64]{2,3,0,1:T(8,128)}) fusion(bf16[2,128,32,128]{3,2,1,0:T(8,128)(2,1)S(1)} %bitcast.84, bf16[64,32,128,1]{2,1,0,3:T(8,128)(2,1)} %bitcast.86, pred[2,128,64]{1,2,0:T(8,128)(4,1)S(1)} %broadcast_or_fusion), kind=kOutput, calls=%fused_computation.83 | convolution fusion | flops 135782400 | bytes 4767744 | tf_op jit(solution)/shard_map/bqhd,jhd->bhqj/dot_general | solution.py:85
  172.4 1.7 fusion.53
  174.1 1.4 copy.98
  176.8 1.7 fusion.52
  180.5 5.2 %bitcast_reduce_fusion = (f32[2,32,128]{2,1,0:T(8,128)S(1)}, f32[2,32,384,128]{3,2,1,0:T(8,128)S(1)}) fusion(pred[2,384]{1,0:T(4,128)(4,1)S(1)} %compare_and_fusion, bf16[2,128,32,128]{3,2,1,0:T(8,128)(2,1)} %bitcast.85, bf16[1,128,32,128]{3,1,2,0:T(8,128)(2,1)} %copy.92, bf16[1,256,32,128]{3,1,2,0:T(8,128)(2,1)} %copy.88, ...), kind=kOutput, calls=%fused_computation.1 | convolution fusion | flops 839901184 | bytes 18907904 | tf_op jit(solution)/shard_map/bqhd,bkhd->bhqk/dot_general | solution.py:53
  185.6 4.0 %fusion.1 = f32[2,32,128]{2,1,0:T(8,128)S(1)} fusion(f32[2,32,384,128]{3,2,1,0:T(8,128)S(1)} %get-tuple-element.18, f32[2,32,128]{2,1,0:T(8,128)S(1)} %get-tuple-element.17, pred[2,384]{1,0:T(4,128)(4,1)S(1)} %compare_and_fusion), kind=kLoop, calls=%fused_computation.4 | loop fusion | flops 12574720 | bytes 12649216 | tf_op jit(solution)/shard_map/reduce_sum | solution.py:66
  191.9 6.1 %fusion.25 = bf16[2,128,32,128]{3,1,2,0:T(8,128)(2,1)S(1)} fusion(f32[32,128,2,128]{1,3,0,2:T(8,128)S(1)} %fusion.37, bf16[1,128,32,128]{3,1,2,0:T(8,128)(2,1)S(1)} %copy-done.5, bf16[1,256,32,128]{3,1,2,0:T(8,128)(2,1)S(1)} %copy-done.2, bf16[1,128,32,128]{3,1,2,0:T(8,128)(2,1)S(1)} %copy-done.6, f32[2,32,384,128]{3,2,1,0:T(8,128)S(1)} %get-tuple-element.18, ...), kind=kOutput, calls=%fused_computation.30 | convolution fusion | flops 847249408 | bytes 23167744 | tf_op jit(solution)/shard_map/bhqk,bkhd->bhqd/dot_general | solution.py:67
  199.3 2.3 %copy.144 = bf16[32,8,32,128]{3,1,2,0:T(8,128)(2,1)} copy(bf16[32,8,32,128]{3,2,1,0:T(8,128)(2,1)S(1)} %bitcast.78) | data formatting | bytes 4194304
  (51 shorter events, 11.2 us)
Async XLA Ops:
  9.3 11.4 %copy-start = (bf16[256,4096]{1,0:T(8,128)(2,1)S(1)}, bf16[256,4096]{1,0:T(8,128)(2,1)}, u32[]{:S(2)}) copy-start(bf16[256,4096]{1,0:T(8,128)(2,1)} %param.6) | copy-start | bytes 6291460
  10.9 161.5 %collective-permute-start.1 = (bf16[2,128,4096]{1,2,0:T(8,128)(2,1)}, bf16[2,128,4096]{1,2,0:T(8,128)(2,1)}, u32[]{:S(2)}, u32[]{:S(2)}) collective-permute-start(bf16[2,128,4096]{1,2,0:T(8,128)(2,1)} %pad_maximum_fusion.1), channel_id=1, source_target_pairs={{1,0},{2,1},{3,2},{4,3},{5,4},{6,5},{7,6},{8,7},{9,8},{10,9},{11,1... | collective-permute-start | bytes 6291464 | tf_op jit(solution)/shard_map/ppermute | solution.py:16
  13.7 7.5 %copy-start.1 = (bf16[256,4096]{1,0:T(8,128)(2,1)S(1)}, bf16[256,4096]{1,0:T(8,128)(2,1)}, u32[]{:S(2)}) copy-start(bf16[256,4096]{1,0:T(8,128)(2,1)} %param.7) | copy-start | bytes 6291460
  13.7 163.0 %collective-permute-start = (bf16[2,128,4096]{1,2,0:T(8,128)(2,1)}, bf16[2,128,4096]{1,2,0:T(8,128)(2,1)}, u32[]{:S(2)}, u32[]{:S(2)}) collective-permute-start(bf16[2,128,4096]{1,2,0:T(8,128)(2,1)} %pad_maximum_fusion), channel_id=1, source_target_pairs={{0,1},{1,2},{2,3},{3,4},{4,5},{5,6},{6,7},{7,8},{8,9},{9,10},{10,1... | collective-permute-start | bytes 6291464 | tf_op jit(solution)/shard_map/ppermute | solution.py:16
  140.6 27.6 %copy-start.7 = (s32[2,32]{1,0:T(2,128)S(1)}, s32[2,32]{1,0:T(2,128)}, u32[]{:S(2)}) copy-start(s32[2,32]{1,0:T(2,128)} %param.9) | copy-start | bytes 772
  140.6 27.7 %copy-start.8 = (s32[2]{0:T(128)S(1)}, s32[2]{0:T(128)}, u32[]{:S(2)}) copy-start(s32[2]{0:T(128)} %param.8) | copy-start | bytes 28
  142.7 29.7 %copy-start.3 = (bf16[32,8,32,128]{3,2,1,0:T(8,128)(2,1)}, bf16[32,8,32,128]{3,2,1,0:T(8,128)(2,1)S(1)}, u32[]{:S(2)}) copy-start(bf16[32,8,32,128]{3,2,1,0:T(8,128)(2,1)S(1)} %copy.115) | copy-start | bytes 6291460
  185.6 4.1 %copy-start.4 = (f32[2,32,128,64]{2,3,0,1:T(8,128)S(1)}, f32[2,32,128,64]{2,3,0,1:T(8,128)}, u32[]{:S(2)}) copy-start(f32[2,32,128,64]{2,3,0,1:T(8,128)} %get-tuple-element.20) | copy-start | bytes 6291460
  189.7 1.6 copy-start.2
  189.7 1.8 copy-start.5
  189.7 2.2 %copy-start.6 = (bf16[1,128,32,128]{3,1,2,0:T(8,128)(2,1)S(1)}, bf16[1,128,32,128]{3,1,2,0:T(8,128)(2,1)}, u32[]{:S(2)}) copy-start(bf16[1,128,32,128]{3,1,2,0:T(8,128)(2,1)} %copy.95) | copy-start | bytes 3145732
where the time goes:
time: 202 us
  blocking collectives  129 us (64%)
  local copies, waits for them, and re-layouts  36.7 us (18%)
  matrix products  15.8 us (8%)
  other arithmetic  11.8 us (6%)
  starting transfers between devices  8.25 us (4%)
    all_gather x1, blocking collectives, shards(): lax.all_gather(summary_keys, 'seq', axis=0, tiled=True)  82.1 us
    all_gather x1, blocking collectives, shards(): piece_keys = lax.all_gather(group_keys, 'grp', axis=0, tiled=True)  23.4 us
    all_gather x1, blocking collectives, shards(): piece_values = lax.all_gather(group_values, 'grp', axis=0, tiled=True)  18.9 us
    unnamed x28, local copies, waits for them, and re-layouts  16.3 us
    ppermute x2, starting transfers between devices, shifted(): return lax.ppermute(value, axis, pairs)  8.25 us
    concatenate x3, local copies, waits for them, and re-layouts, shards(): wide_values = jnp.concatenate([from_left[1], values, from_right[1]], axis=0)  6.82 us
    dot_general x1, matrix products, shards(): jnp.einsum('bhqk,bkhd->bhqd', weights.astype(jnp.bfloat16), window_values...  6.06 us
    dot_general x1, matrix products, shards(): jnp.einsum('bqhd,bkhd->bhqk', query_blocks, window_keys, preferred_elemen...  5.16 us
  transfers between devices with their start and end apart: 2, of which 0 were waited for; matrix products, arithmetic and copies ran while one was open for 14% of the time, Pallas kernels for 0%

commit v1 on v0

v1 whole, which is shorter than its diff:
```python
import functools
import math

import jax
import jax.numpy as jnp
from jax import lax
from jax.experimental import pallas as pl
from jax.experimental.pallas import tpu as pltpu
from jax.sharding import PartitionSpec as P

HEAD_DIM = 128
BLOCK = 128
CHUNK_HEADS = 2
POOL_HEADS = 8
MESH = pl.DeviceIdType.MESH


def dot_t(a, b):
    return lax.dot_general(a, b, (((1,), (1,)), ((), ())), preferred_element_type=jnp.float32)


def dot(a, b):
    return jnp.dot(a, b, preferred_element_type=jnp.float32)


def kernel(
    groups, seqs, pos_ref, layout_ref, q_hbm, k_hbm, v_hbm, out_hbm,
    q, k, v, out, halo, gathered, own, wide, bias,
    load_sem, store_sem, send_sem, recv_sem, seq_send, seq_recv, grp_send, grp_recv,
):
    rows, width = q.shape
    heads = width // HEAD_DIM
    blocks = rows // BLOCK
    devices = groups * seqs
    total_blocks = devices * blocks
    step_cols = CHUNK_HEADS * HEAD_DIM
    chunks = heads // CHUNK_HEADS
    stages = groups.bit_length() - 1
    near = 2 * seqs

    g, s = lax.axis_index("grp"), lax.axis_index("seq")
    me = g * seqs + s
    has_left, has_right = me > 0, me < devices - 1
    left, right = lax.max(me - 1, 0), lax.min(me + 1, devices - 1)

    def coords(position):
        return (position // seqs, position % seqs)

    left_near = has_left & (me % near != 0)
    right_near = has_right & ((me + 1) % near != 0)
    left_far = has_left & (me % near == 0)
    right_far = has_right & ((me + 1) % near == 0)

    loads = [
        pltpu.make_async_copy(src, dst, load_sem.at[i])
        for i, (src, dst) in enumerate(((k_hbm, k), (v_hbm, v), (q_hbm, q)))
    ]
    for load in loads:
        load.start()

    barrier = pltpu.get_barrier_semaphore()

    def signal(device):
        pl.semaphore_signal(barrier, inc=1, device_id=device, device_id_type=MESH)

    @pl.when(has_left)
    def _():
        signal(coords(left))

    @pl.when(has_right)
    def _():
        signal(coords(right))

    for o in range(1, seqs):
        signal((g, lax.rem(s + o, seqs)))

    def partner(stage):
        size = 1 << stage
        bit = (g // size) % 2
        return g + size * (1 - 2 * bit)

    for stage in range(stages):
        signal((partner(stage), s))
    pl.semaphore_wait(
        barrier, seqs - 1 + stages + has_left.astype(jnp.int32) + has_right.astype(jnp.int32)
    )

    def edge(side, kv, c):
        src = (k_hbm, v_hbm)[kv]
        cols = pl.ds(pl.multiple_of(c * step_cols, step_cols), step_cols)
        first = rows - BLOCK if side == 0 else 0
        return pltpu.make_async_remote_copy(
            src_ref=src.at[pl.ds(first, BLOCK), cols],
            dst_ref=halo.at[side, kv, :, cols],
            send_sem=send_sem.at[side, kv, c],
            recv_sem=recv_sem.at[side, kv, c],
            device_id=coords(right if side == 0 else left),
            device_id_type=MESH,
        )

    def send_edges(side, when, lo, hi):
        @pl.when(when)
        def _():
            def body(c, carry):
                for kv in range(2):
                    edge(side, kv, c).start()
                return carry

            lax.fori_loop(lo, hi, body, 0)

    def send_both(when_right, when_left, lo, hi):
        both = when_right & when_left

        @pl.when(both)
        def _():
            def body(c, carry):
                for side in range(2):
                    for kv in range(2):
                        edge(side, kv, c).start()
                return carry

            lax.fori_loop(lo, hi, body, 0)

        send_edges(0, when_right & jnp.logical_not(when_left), lo, hi)
        send_edges(1, when_left & jnp.logical_not(when_right), lo, hi)

    send_both(right_near, left_near, 0, 1)

    loads[0].wait()
    loads[1].wait()
    picks = (
        lax.broadcasted_iota(jnp.int32, (16, rows), 1) // BLOCK
        == lax.broadcasted_iota(jnp.int32, (16, rows), 0)
    ).astype(jnp.bfloat16)

    def pool(step, carry):
        for i in range(POOL_HEADS):
            h = step * POOL_HEADS + i
            cols = pl.ds(pl.multiple_of(h * HEAD_DIM, HEAD_DIM), HEAD_DIM)
            for kv, src in enumerate((k, v)):
                mean = dot(picks, src[:, cols])[:8] * (1.0 / BLOCK)
                spread = jnp.mean(mean * mean, axis=-1, keepdims=True)
                scaled = mean / jnp.sqrt(spread + 1e-06)
                for b in range(blocks):
                    own[pl.ds((kv * blocks + b) * heads + h, 1), :] = scaled[b : b + 1]
        return carry

    lax.fori_loop(0, heads // POOL_HEADS, pool, 0)
    gathered[me] = own[...].astype(jnp.bfloat16)

    def seq_copy(o):
        return pltpu.make_async_remote_copy(
            src_ref=gathered.at[pl.ds(me, 1)],
            dst_ref=gathered.at[pl.ds(me, 1)],
            send_sem=seq_send.at[o],
            recv_sem=seq_recv.at[o],
            device_id=(g, lax.rem(s + o, seqs)),
            device_id_type=MESH,
        )

    for o in range(1, seqs):
        seq_copy(o).start()

    send_both(right_near, left_near, 1, chunks)

    ids = lax.broadcasted_iota(jnp.int32, (BLOCK, total_blocks), 1)
    spots = lax.broadcasted_iota(jnp.int32, (BLOCK, total_blocks), 0)
    for b in range(blocks):
        seen = spots == pos_ref[b]
        for link in range(layout_ref.shape[1]):
            seen = seen | (ids == layout_ref[b, link])
        bias[b * BLOCK : (b + 1) * BLOCK, :] = jnp.where(seen, 0.0, -jnp.inf)

    @pl.when(jnp.logical_not(has_left))
    def _():
        halo[0] = jnp.zeros(halo.shape[1:], halo.dtype)

    @pl.when(jnp.logical_not(has_right))
    def _():
        halo[1] = jnp.zeros(halo.shape[1:], halo.dtype)

    for o in range(1, seqs):
        seq_copy(o).wait()

    def grp_copy(stage):
        size = (1 << stage) * seqs
        first = (g // (1 << stage)) * size
        return pltpu.make_async_remote_copy(
            src_ref=gathered.at[pl.ds(first, size)],
            dst_ref=gathered.at[pl.ds(first, size)],
            send_sem=grp_send.at[stage],
            recv_sem=grp_recv.at[stage],
            device_id=(partner(stage), s),
            device_id_type=MESH,
        )

    for stage in range(stages):
        grp_copy(stage).start()
        if stage == stages - 1:
            send_both(right_far, left_far, 0, chunks)
        grp_copy(stage).wait()

    def widen(d, carry):
        spread = blocks * heads
        at = pl.ds(pl.multiple_of(d * spread, spread), spread)
        for kv in range(2):
            wide[kv, at, :] = gathered[d, kv * spread : (kv + 1) * spread].astype(jnp.float32)
        return carry

    lax.fori_loop(0, devices, widen, 0)
    loads[2].wait()

    factor = math.log2(math.e) / math.sqrt(HEAD_DIM)
    left_bias = jnp.where(has_left, 0.0, -jnp.inf)
    right_bias = jnp.where(has_right, 0.0, -jnp.inf)

    def store(c):
        cols = pl.ds(pl.multiple_of(c * step_cols, step_cols), step_cols)
        return pltpu.make_async_copy(out.at[:, cols], out_hbm.at[:, cols], store_sem.at[c])

    def attend(c, carry):
        for side, there in ((0, has_left), (1, has_right)):
            @pl.when(there)
            def _(side=side):
                for kv in range(2):
                    edge(side, kv, c).wait_recv()

        for i in range(CHUNK_HEADS):
            h = c * CHUNK_HEADS + i
            cols = pl.ds(pl.multiple_of(h * HEAD_DIM, HEAD_DIM), HEAD_DIM)
            rows_of = pl.ds(h, total_blocks, stride=heads)
            qh, kh, vh = q[:, cols], k[:, cols], v[:, cols]
            sk = wide[0, rows_of, :].astype(jnp.bfloat16)
            sv = wide[1, rows_of, :].astype(jnp.bfloat16)
            kl, vl = halo[0, 0, :, cols], halo[0, 1, :, cols]
            kr, vr = halo[1, 0, :, cols], halo[1, 1, :, cols]
            s_own = dot_t(qh, kh)
            if blocks > 2:
                gap = (
                    lax.broadcasted_iota(jnp.int32, (rows, rows), 0) // BLOCK
                    - lax.broadcasted_iota(jnp.int32, (rows, rows), 1) // BLOCK
                )
                s_own = jnp.where(jnp.abs(gap) <= 1, s_own, -jnp.inf)
            s_left = dot_t(qh[:BLOCK], kl) + left_bias
            s_right = dot_t(qh[rows - BLOCK :], kr) + right_bias
            s_sum = dot_t(qh, sk) + bias[...]
            middle = [jnp.full((rows - 2 * BLOCK, BLOCK), -jnp.inf)] if blocks > 2 else []
            s_halo = jnp.concatenate([s_left, *middle, s_right], axis=0)
            peak = jnp.maximum(
                jnp.max(s_sum, axis=-1, keepdims=True),
                jnp.maximum(
                    jnp.max(s_own, axis=-1, keepdims=True),
                    jnp.max(s_halo, axis=-1, keepdims=True),
                ),
            )
            w_own = jnp.exp2((s_own - peak) * factor)
            w_halo = jnp.exp2((s_halo - peak) * factor)
            w_sum = jnp.exp2((s_sum - peak) * factor)
            total = (
                jnp.sum(w_own, axis=-1, keepdims=True)
                + jnp.sum(w_halo, axis=-1, keepdims=True)
                + jnp.sum(w_sum, axis=-1, keepdims=True)
            )
            r_halo = w_halo.astype(jnp.bfloat16)
            acc = dot(w_own.astype(jnp.bfloat16), vh) + dot(w_sum.astype(jnp.bfloat16), sv)
            middle = [jnp.zeros((rows - 2 * BLOCK, HEAD_DIM), jnp.float32)] if blocks > 2 else []
            acc = acc + jnp.concatenate(
                [dot(r_halo[:BLOCK], vl), *middle, dot(r_halo[rows - BLOCK :], vr)], axis=0
            )
            out[:, cols] = (acc / total).astype(jnp.bfloat16)
        store(c).start()
        return carry

    lax.fori_loop(0, chunks, attend, 0)

    def finish(c, carry):
        store(c).wait()
        for side, there in ((0, has_right), (1, has_left)):
            @pl.when(there)
            def _(side=side):
                for kv in range(2):
                    edge(side, kv, c).wait_send()
        return carry

    lax.fori_loop(0, chunks, finish, 0)


def solution(mesh):
    groups, seqs = mesh.shape["grp"], mesh.shape["seq"]
    assert groups & (groups - 1) == 0

    def shards(queries, keys, values, global_pos, layout):
        rows, width = queries.shape
        blocks, heads = rows // BLOCK, width // HEAD_DIM
        devices = groups * seqs
        chunks = heads // CHUNK_HEADS
        stages = groups.bit_length() - 1
        return pl.pallas_call(
            functools.partial(kernel, groups, seqs),
            out_shape=jax.ShapeDtypeStruct((rows, width), jnp.bfloat16),
            in_specs=[pl.BlockSpec(memory_space=pltpu.SMEM)] * 2
            + [pl.BlockSpec(memory_space=pl.ANY)] * 3,
            out_specs=pl.BlockSpec(memory_space=pl.ANY),
            scratch_shapes=[
                pltpu.VMEM((rows, width), jnp.bfloat16),
                pltpu.VMEM((rows, width), jnp.bfloat16),
                pltpu.VMEM((rows, width), jnp.bfloat16),
                pltpu.VMEM((rows, width), jnp.bfloat16),
                pltpu.VMEM((2, 2, BLOCK, width), jnp.bfloat16),
                pltpu.VMEM((devices, 2 * blocks * heads, HEAD_DIM), jnp.bfloat16),
                pltpu.VMEM((2 * blocks * heads, HEAD_DIM), jnp.float32),
                pltpu.VMEM((2, devices * blocks * heads, HEAD_DIM), jnp.float32),
                pltpu.VMEM((rows, devices * blocks), jnp.float32),
                pltpu.SemaphoreType.DMA((3,)),
                pltpu.SemaphoreType.DMA((chunks,)),
                pltpu.SemaphoreType.DMA((2, 2, chunks)),
                pltpu.SemaphoreType.DMA((2, 2, chunks)),
                pltpu.SemaphoreType.DMA((seqs,)),
                pltpu.SemaphoreType.DMA((seqs,)),
                pltpu.SemaphoreType.DMA((max(stages, 1),)),
                pltpu.SemaphoreType.DMA((max(stages, 1),)),
            ],
            compiler_params=pltpu.CompilerParams(
                collective_id=0, has_side_effects=True, vmem_limit_bytes=60 * 1024 * 1024
            ),
        )(global_pos, layout, queries, keys, values)

    both = ("grp", "seq")
    in_specs = (P(both, None), P(both, None), P(both, None), P(both), P(both, None))
    return jax.shard_map(
        shards, mesh=mesh, in_specs=in_specs, out_specs=P(both, None), check_vma=False
    )
```

time: 202 us -> 104 us (0.51)
  blocking collectives: 129 us -> 0 us
  Pallas kernels: 0 us -> 101 us
  local copies, waits for them, and re-layouts: 36.7 us -> 3.13 us
  matrix products: 15.8 us -> 0 us
  other arithmetic: 11.8 us -> 0 us
  starting transfers between devices: 8.25 us -> 0 us
    all_gather x4 -> x0, blocking collectives: 129 us -> none  [the longest x1 82.1 us: shards(): lax.all_gather(summary_keys, 'seq', axis=0, tiled=True)]
    pallas_call x0 -> x1, Pallas kernels: none -> 101 us  [shards(): pl.pallas_call(functools.partial(kernel, groups, seqs), out_shape=jax.Sha...]
    dot_general x4 -> x0, matrix products: 15.8 us -> none  [the longest x1 6.06 us: shards(): jnp.einsum('bhqk,bkhd->bhqd', weights.astype(jnp.bfloat16), window_values...]
    unnamed x28 -> x1, local copies, waits for them, and re-layouts: 16.3 us -> 3.13 us
    concatenate x6 -> x0, local copies, waits for them, and re-layouts: 11.7 us -> none  [the longest x3 6.82 us: shards(): wide_values = jnp.concatenate([from_left[1], values, from_right[1]], axis=0)]
    ppermute x2 -> x0, starting transfers between devices: 8.25 us -> none  [shifted(): return lax.ppermute(value, axis, pairs)]
    reduce_sum x6 -> x0, other arithmetic: 5.25 us -> none  [the longest x1 3.99 us: shards(): totals = jnp.sum(weights, axis=-1)]
    slice x2 -> x0, local copies, waits for them, and re-layouts: 3.36 us -> none  [shards(): wide_values = jnp.concatenate([from_left[1], values, from_right[1]], axis=0)]
  transfers between devices with their start and end apart: 2 -> 0, of which waited for: 0 -> 0; matrix products, arithmetic and copies ran while one was open for 14% -> 0% of each run, Pallas kernels for 0% -> 0%
where the time goes in v1:
time: 104 us
  Pallas kernels  101 us (97%)
  local copies, waits for them, and re-layouts  3.13 us (3%)
    pallas_call x1, Pallas kernels, shards(): pl.pallas_call(functools.partial(kernel, groups, seqs), out_shape=jax.Sha...  101 us
    unnamed x1, local copies, waits for them, and re-layouts  3.13 us

profile of v1, /device:TPU:0, one launch (start us, length us, event | category | flops | bytes accessed | tf_op | source)
XLA Modules:
  0.0 103.8 jit_solution(9021181025804225823)
XLA Ops:
  0.0 100.6 %shard_map.55 = bf16[256,4096]{1,0:T(8,128)(2,1)} custom-call(s32[2]{0:T(128)} %pos_ref.1, s32[2,32]{1,0:T(2,128)} %layout_ref.1, bf16[256,4096]{1,0:T(8,128)(2,1)} %q_hbm.1, bf16[256,4096]{1,0:T(8,128)(2,1)} %k_hbm.1, bf16[256,4096]{1,0:T(8,128)(2,1)} %v_hbm.1), custom_call_target="tpu_custom_call" | custom-call | tf_op jit(solution)/shard_map/pallas_call | solution.py:298
  100.7 3.1 %copy.7 = bf16[256,4096]{1,0:T(8,128)(2,1)} copy(bf16[256,4096]{1,0:T(8,128)(2,1)} %shard_map.55) | data formatting | bytes 4194304

commit v2 on v1

--- a/solution.py
+++ b/solution.py
@@ -11,6 +11,7 @@
 HEAD_DIM = 128
 BLOCK = 128
 CHUNK_HEADS = 2
+EARLY_CHUNKS = 4
 POOL_HEADS = 8
 MESH = pl.DeviceIdType.MESH
 
@@ -24,9 +25,9 @@
 
 
 def kernel(
-    groups, seqs, pos_ref, layout_ref, q_hbm, k_hbm, v_hbm, out_hbm,
-    q, k, v, out, halo, gathered, own, wide, bias,
-    load_sem, store_sem, send_sem, recv_sem, seq_send, seq_recv, grp_send, grp_recv,
+    groups, seqs, pos_hbm, layout_hbm, q_hbm, k_hbm, v_hbm, out,
+    pos_ref, layout_ref, q, k, v, halo, gathered, own, wide, bias,
+    load_sem, send_sem, recv_sem, seq_send, seq_recv, grp_send, grp_recv,
 ):
     rows, width = q.shape
     heads = width // HEAD_DIM
@@ -53,7 +54,7 @@
 
     loads = [
         pltpu.make_async_copy(src, dst, load_sem.at[i])
-        for i, (src, dst) in enumerate(((k_hbm, k), (v_hbm, v), (q_hbm, q)))
+        for i, (src, dst) in enumerate(((k_hbm, k), (v_hbm, v), (q_hbm, q), (pos_hbm, pos_ref), (layout_hbm, layout_ref)))
     ]
     for load in loads:
         load.start()
@@ -124,7 +125,10 @@
         send_edges(0, when_right & jnp.logical_not(when_left), lo, hi)
         send_edges(1, when_left & jnp.logical_not(when_right), lo, hi)
 
-    send_both(right_near, left_near, 0, 1)
+    early = min(EARLY_CHUNKS, chunks)
+    later = (early + chunks) // 2
+    send_both(right_near, left_near, 0, early)
+    send_both(right_far, left_far, 0, early)
 
     loads[0].wait()
     loads[1].wait()
@@ -161,8 +165,10 @@
     for o in range(1, seqs):
         seq_copy(o).start()
 
-    send_both(right_near, left_near, 1, chunks)
-
+    send_both(right_near, left_near, early, chunks)
+
+    loads[3].wait()
+    loads[4].wait()
     ids = lax.broadcasted_iota(jnp.int32, (BLOCK, total_blocks), 1)
     spots = lax.broadcasted_iota(jnp.int32, (BLOCK, total_blocks), 0)
     for b in range(blocks):
@@ -196,8 +202,10 @@
 
     for stage in range(stages):
         grp_copy(stage).start()
+        if stage == stages - 2:
+            send_both(right_far, left_far, early, later)
         if stage == stages - 1:
-            send_both(right_far, left_far, 0, chunks)
+            send_both(right_far, left_far, later if stages > 1 else early, chunks)
         grp_copy(stage).wait()
 
     def widen(d, carry):
@@ -213,10 +221,6 @@
     factor = math.log2(math.e) / math.sqrt(HEAD_DIM)
     left_bias = jnp.where(has_left, 0.0, -jnp.inf)
     right_bias = jnp.where(has_right, 0.0, -jnp.inf)
-
-    def store(c):
-        cols = pl.ds(pl.multiple_of(c * step_cols, step_cols), step_cols)
-        return pltpu.make_async_copy(out.at[:, cols], out_hbm.at[:, cols], store_sem.at[c])
 
     def attend(c, carry):
         for side, there in ((0, has_left), (1, has_right)):
@@ -268,13 +272,11 @@
                 [dot(r_halo[:BLOCK], vl), *middle, dot(r_halo[rows - BLOCK :], vr)], axis=0
             )
             out[:, cols] = (acc / total).astype(jnp.bfloat16)
-        store(c).start()
         return carry
 
     lax.fori_loop(0, chunks, attend, 0)
 
     def finish(c, carry):
-        store(c).wait()
         for side, there in ((0, has_right), (1, has_left)):
             @pl.when(there)
             def _(side=side):
@@ -295,14 +297,20 @@
         devices = groups * seqs
         chunks = heads // CHUNK_HEADS
         stages = groups.bit_length() - 1
+        summaries = devices * blocks * width
+        limit = 2 * (4 * rows + 4 * BLOCK) * width + 12 * summaries + (8 << 20)
+        operands = [
+            pltpu.with_memory_space_constraint(a, pltpu.HBM)
+            for a in (global_pos, layout, queries, keys, values)
+        ]
         return pl.pallas_call(
             functools.partial(kernel, groups, seqs),
-            out_shape=jax.ShapeDtypeStruct((rows, width), jnp.bfloat16),
-            in_specs=[pl.BlockSpec(memory_space=pltpu.SMEM)] * 2
-            + [pl.BlockSpec(memory_space=pl.ANY)] * 3,
-            out_specs=pl.BlockSpec(memory_space=pl.ANY),
+            out_shape=pltpu.VMEM((rows, width), jnp.bfloat16),
+            in_specs=[pl.BlockSpec(memory_space=pltpu.HBM)] * 5,
+            out_specs=pl.BlockSpec(memory_space=pltpu.VMEM),
             scratch_shapes=[
-                pltpu.VMEM((rows, width), jnp.bfloat16),
+                pltpu.SMEM(global_pos.shape, jnp.int32),
+                pltpu.SMEM(layout.shape, jnp.int32),
                 pltpu.VMEM((rows, width), jnp.bfloat16),
                 pltpu.VMEM((rows, width), jnp.bfloat16),
                 pltpu.VMEM((rows, width), jnp.bfloat16),
@@ -311,8 +319,7 @@
                 pltpu.VMEM((2 * blocks * heads, HEAD_DIM), jnp.float32),
                 pltpu.VMEM((2, devices * blocks * heads, HEAD_DIM), jnp.float32),
                 pltpu.VMEM((rows, devices * blocks), jnp.float32),
-                pltpu.SemaphoreType.DMA((3,)),
-                pltpu.SemaphoreType.DMA((chunks,)),
+                pltpu.SemaphoreType.DMA((5,)),
                 pltpu.SemaphoreType.DMA((2, 2, chunks)),
                 pltpu.SemaphoreType.DMA((2, 2, chunks)),
                 pltpu.SemaphoreType.DMA((seqs,)),
@@ -321,9 +328,9 @@
                 pltpu.SemaphoreType.DMA((max(stages, 1),)),
             ],
             compiler_params=pltpu.CompilerParams(
-                collective_id=0, has_side_effects=True, vmem_limit_bytes=60 * 1024 * 1024
+                collective_id=0, has_side_effects=True, vmem_limit_bytes=limit
             ),
-        )(global_pos, layout, queries, keys, values)
+        )(*operands)
 
     both = ("grp", "seq")
     in_specs = (P(both, None), P(both, None), P(both, None), P(both), P(both, None))

time: 104 us -> 101 us (0.971)
  local copies, waits for them, and re-layouts: 3.13 us -> 1.32 us
  Pallas kernels: 101 us -> 99.3 us
    unnamed x1, local copies, waits for them, and re-layouts: 3.13 us -> 1.32 us
    pallas_call x1, Pallas kernels: 101 us -> 99.3 us  [shards(): pl.pallas_call(functools.partial(kernel, groups, seqs), out_shape=pltpu.V...]
where the time goes in v2:
time: 101 us
  Pallas kernels  99.3 us (98%)
  local copies, waits for them, and re-layouts  1.32 us (1%)
    pallas_call x1, Pallas kernels, shards(): pl.pallas_call(functools.partial(kernel, groups, seqs), out_shape=pltpu.V...  99.3 us

profile of v2, /device:TPU:0, one launch (start us, length us, event | category | flops | bytes accessed | tf_op | source)
XLA Modules:
  0.0 100.6 jit_solution(15946530991738166780)
XLA Ops:
  0.0 99.3 %shard_map.55 = bf16[256,4096]{1,0:T(8,128)(2,1)S(1)} custom-call(s32[2]{0:T(128)} %pos_hbm.1, s32[2,32]{1,0:T(2,128)} %layout_hbm.1, bf16[256,4096]{1,0:T(8,128)(2,1)} %q_hbm.1, bf16[256,4096]{1,0:T(8,128)(2,1)} %k_hbm.1, bf16[256,4096]{1,0:T(8,128)(2,1)} %v_hbm.1), custom_call_target="tpu_custom_call" | custom-call | tf_op jit(solution)/shard_map/pallas_call | solution.py:306
  99.3 1.3 %copy.7 = bf16[256,4096]{1,0:T(8,128)(2,1)} copy(bf16[256,4096]{1,0:T(8,128)(2,1)S(1)} %shard_map.55) | data formatting | bytes 4194304

commit v3 on v2

--- a/solution.py
+++ b/solution.py
@@ -56,9 +56,6 @@
         pltpu.make_async_copy(src, dst, load_sem.at[i])
         for i, (src, dst) in enumerate(((k_hbm, k), (v_hbm, v), (q_hbm, q), (pos_hbm, pos_ref), (layout_hbm, layout_ref)))
     ]
-    for load in loads:
-        load.start()
-
     barrier = pltpu.get_barrier_semaphore()
 
     def signal(device):
@@ -82,12 +79,14 @@
 
     for stage in range(stages):
         signal((partner(stage), s))
+    for load in loads:
+        load.start()
     pl.semaphore_wait(
         barrier, seqs - 1 + stages + has_left.astype(jnp.int32) + has_right.astype(jnp.int32)
     )
 
     def edge(side, kv, c):
-        src = (k_hbm, v_hbm)[kv]
+        src = (k, v)[kv]
         cols = pl.ds(pl.multiple_of(c * step_cols, step_cols), step_cols)
         first = rows - BLOCK if side == 0 else 0
         return pltpu.make_async_remote_copy(
@@ -125,13 +124,12 @@
         send_edges(0, when_right & jnp.logical_not(when_left), lo, hi)
         send_edges(1, when_left & jnp.logical_not(when_right), lo, hi)
 
+    loads[0].wait()
+    loads[1].wait()
     early = min(EARLY_CHUNKS, chunks)
     later = (early + chunks) // 2
     send_both(right_near, left_near, 0, early)
-    send_both(right_far, left_far, 0, early)
-
-    loads[0].wait()
-    loads[1].wait()
+
     picks = (
         lax.broadcasted_iota(jnp.int32, (16, rows), 1) // BLOCK
         == lax.broadcasted_iota(jnp.int32, (16, rows), 0)
@@ -203,7 +201,7 @@
     for stage in range(stages):
         grp_copy(stage).start()
         if stage == stages - 2:
-            send_both(right_far, left_far, early, later)
+            send_both(right_far, left_far, 0, later)
         if stage == stages - 1:
             send_both(right_far, left_far, later if stages > 1 else early, chunks)
         grp_copy(stage).wait()

time: 101 us -> 101 us (level)
  no operation moved by 1% of the time
where the time goes in v3:
time: 101 us; the launch traced here: 100 us
  Pallas kernels  99 us (98%)
  local copies, waits for them, and re-layouts  1.32 us (1%)
    pallas_call x1, Pallas kernels, shards(): pl.pallas_call(functools.partial(kernel, groups, seqs), out_shape=pltpu.V...  99 us

profile of v3, /device:TPU:0, one launch (start us, length us, event | category | flops | bytes accessed | tf_op | source)
XLA Modules:
  0.0 100.4 jit_solution(11832801148701795260)
XLA Ops:
  0.0 99.0 %shard_map.55 = bf16[256,4096]{1,0:T(8,128)(2,1)S(1)} custom-call(s32[2]{0:T(128)} %pos_hbm.1, s32[2,32]{1,0:T(2,128)} %layout_hbm.1, bf16[256,4096]{1,0:T(8,128)(2,1)} %q_hbm.1, bf16[256,4096]{1,0:T(8,128)(2,1)} %k_hbm.1, bf16[256,4096]{1,0:T(8,128)(2,1)} %v_hbm.1), custom_call_target="tpu_custom_call" | custom-call | tf_op jit(solution)/shard_map/pallas_call | solution.py:304
  99.1 1.3 %copy.7 = bf16[256,4096]{1,0:T(8,128)(2,1)} copy(bf16[256,4096]{1,0:T(8,128)(2,1)S(1)} %shard_map.55) | data formatting | bytes 4194304
